TPU v7x, 32 devices: a whole 2x2x4 slice. The times are simulated.
32 devices in a mesh: groups: 2 (over y), blk: 4 (over z), tok: 4 (over x, core).
Axes of the slice: x: 2, y: 2, z: 4, core: 2. Of those that a mesh axis runs over, the one named last changes fastest.
Arguments:
- tokens: bfloat16 [2048, 3584], P(('groups', 'blk', 'tok')), parts along dimension 0, may hold values from -6 to 6
- expert_ids: int32 [2048, 1], P(('groups', 'blk', 'tok')), parts along dimension 0, may hold values from 0 to 1; in each aligned block of 256 rows (0 to 255, 256 to 511, ...) at most 192 rows name the same one
- gate_values: float32 [2048, 1], P(('groups', 'blk', 'tok')), parts along dimension 0, may hold values from 0.2 to 1
- w_gate: bfloat16 [2, 3584, 1024], P(None, 'blk', 'tok'), may hold values from -0.09375 to 0.09375
- w_up: bfloat16 [2, 3584, 1024], P(None, 'blk', 'tok'), may hold values from -0.09375 to 0.09375
- w_down: bfloat16 [2, 1024, 3584], P(None, 'tok', 'blk'), may hold values from -0.1875 to 0.1875
Outputs:
- mixed: bfloat16 [2048, 3584], P(('groups', 'blk', 'tok')), parts along dimension 0
There are 2 independent parts, one for each index of `groups`. A program takes and returns all parts, laid end to end along the dimension named above; an argument that names none is the same for every part. Nothing has to cross between parts.
Inputs may be any that keep to these rules, and one draw needn't show every extreme that they name: `expert_ids`: in each aligned block of 256 rows (the tokens of one index of blk), no expert is named by more than 192 rows, and in every draw some expert reaches 192 in some block.
All inputs are finite; a program needn't handle non-finite values.
Results may differ from a plain program's by a relative error of at most 0.005.
Values may be sent and summed in bfloat16 or wider, within the bound.
A program may use at most 64 MiB of HBM per device.

v0:
```python
import jax
import jax.numpy as jnp
from jax import lax
from jax.sharding import PartitionSpec as P


def body(tokens, expert_ids, gate_values, w_gate, w_up, w_down):
    group_rows = lax.all_gather(tokens, "tok", axis=0, tiled=True)
    group_routes = lax.all_gather(expert_ids, "tok", axis=0, tiled=True)[:, 0]
    experts = w_gate.shape[0]
    count_rows = group_rows.shape[0]
    capacity = 3 * count_rows // 4
    expert_range = jnp.arange(experts, dtype=jnp.int32)
    onehot = (group_routes[:, None] == expert_range[None, :]).astype(jnp.int32)
    slot_rank = jnp.sum((jnp.cumsum(onehot, axis=0) - onehot) * onehot, axis=1)
    expert_match = group_routes[None, None, :] == expert_range[:, None, None]
    slot_match = slot_rank[None, None, :] == jnp.arange(capacity, dtype=jnp.int32)[None, :, None]
    dispatch = (expert_match & slot_match).astype(jnp.bfloat16)
    slots = jnp.einsum(
        "esg,gd->esd", dispatch, group_rows, preferred_element_type=jnp.float32
    ).astype(jnp.bfloat16)

    def add_part(weights):
        return jnp.einsum("esd,edf->esf", slots, weights, preferred_element_type=jnp.float32)

    gate_sum = add_part(lax.all_gather(w_gate, "blk", axis=1, tiled=True))
    up_sum = add_part(lax.all_gather(w_up, "blk", axis=1, tiled=True))
    hidden = (jax.nn.silu(gate_sum) * up_sum).astype(jnp.bfloat16)
    slot_out = jnp.einsum(
        "esf,efd->esd",
        hidden,
        lax.all_gather(w_down, "blk", axis=2, tiled=True),
        preferred_element_type=jnp.float32,
    )
    flat_rows = slot_out.reshape(experts * capacity, slot_out.shape[2])
    position = group_routes * capacity + slot_rank
    partial_value = jnp.take(flat_rows, position, axis=0)
    summed = lax.psum_scatter(partial_value, "tok", scatter_dimension=0, tiled=True)
    return (gate_values * summed).astype(jnp.bfloat16)


def solution(mesh):
    return jax.shard_map(
        body,
        mesh=mesh,
        in_specs=(
            P(("groups", "blk", "tok"), None),
            P(("groups", "blk", "tok"), None),
            P(("groups", "blk", "tok"), None),
            P(None, "blk", "tok"),
            P(None, "blk", "tok"),
            P(None, "tok", "blk"),
        ),
        out_specs=P(("groups", "blk", "tok"), None),
        check_vma=False,
    )
```

profile of v0, /device:TPU:0, one launch (start us, length us, event | category | flops | bytes accessed | tf_op | source)
XLA Modules:
  0.0 318.8 jit_solution(17435977907468834907)
XLA Ops:
  6.5 0.0 all-gather.5.cloned.1.call-start
  6.5 0.7 all-gather.5.cloned.1.call-update
  7.3 0.0 all-gather.7.cloned.1.call-start
  7.3 0.7 all-gather.7.cloned.1.call-update
  8.0 0.0 all-gather.11.cloned.1.call-start
  8.1 0.7 all-gather.11.cloned.1.call-update
  8.7 0.0 all-gather.9.cloned.1.call-start
  8.8 0.5 all-gather.9.cloned.1.call-update
  9.3 0.0 reduce-scatter.2.cloned.1.call-start
  9.4 1.2 dynamic-slice
  11.3 0.8 bitcast_dynamic-update-slice_fusion
  12.0 6.4 %all-reduce = s32[256]{0:T(256)S(1)} all-reduce(s32[256]{0:T(256)S(1)} %bitcast_dynamic-update-slice_fusion), channel_id=1, replica_groups=mesh['groups'=2,'blk'=4,'tok'=4] {'tok'}, use_global_device_ids=true, to_apply=%add | all-reduce | flops 256 | bytes 2048 | tf_op jit(solution)/shard_map/eq | solution.py:14
  18.4 0.6 reduce-window.6
  19.0 0.2 slice_reduce_fusion
  19.2 0.2 reduce-window.9
  19.4 0.1 add_bitcast_fusion
  19.6 13.1 %all-gather.5.cloned.1.call-done = bf16[256,3584]{1,0:T(8,128)(2,1)} async-done(((bf16[64,3584]{1,0:T(8,128)(2,1)}), bf16[256,3584]{1,0:T(8,128)(2,1)}) %all-gather.5.cloned.1.call-update) | async-done | bytes 1835024 | tf_op jit(solution)/shard_map/all_gather | solution.py:8
  32.7 2.4 convolution_convert_fusion
  35.1 71.3 %all-gather.7.cloned.1.call-done = bf16[2,3584,256]{2,1,0:T(8,128)(2,1)} async-done(((bf16[2,896,256]{2,1,0:T(8,128)(2,1)}), bf16[2,3584,256]{2,1,0:T(8,128)(2,1)}) %all-gather.7.cloned.1.call-update) | async-done | bytes 3670032 | tf_op jit(solution)/shard_map/all_gather | solution.py:26
  106.4 2.9 fusion.16
  109.4 69.4 %all-gather.11.cloned.1.call-done = bf16[2,256,3584]{2,1,0:T(8,128)(2,1)} async-done(((bf16[2,256,896]{2,1,0:T(8,128)(2,1)}), bf16[2,256,3584]{2,1,0:T(8,128)(2,1)}) %all-gather.11.cloned.1.call-update) | async-done | bytes 3670032 | tf_op jit(solution)/shard_map/all_gather | solution.py:32
  178.7 72.1 %all-gather.9.cloned.1.call-done = bf16[2,3584,256]{2,1,0:T(8,128)(2,1)} async-done(((bf16[2,896,256]{2,1,0:T(8,128)(2,1)}), bf16[2,3584,256]{2,1,0:T(8,128)(2,1)}) %all-gather.9.cloned.1.call-update) | async-done | bytes 3670032 | tf_op jit(solution)/shard_map/all_gather | solution.py:27
  250.8 7.2 %fusion.2 = f32[2,192,3584]{2,1,0:T(8,128)} fusion(bf16[2,256,3584]{2,1,0:T(8,128)(2,1)} %all-gather.11.cloned.1.call-done, bf16[2,192,3584]{2,1,0:T(8,128)(2,1)S(1)} %convolution_convert_fusion, bf16[2,3584,256]{2,1,0:T(8,128)(2,1)} %all-gather.9.cloned.1.call-done, f32[2,192,256]{2,1,0:T(8,128)S(1)} %fusion.16), kind=kOutput, calls=%fused_computation.6 | convolution fusion | flops 1409875968 | bytes 15990784 | tf_op jit(solution)/shard_map/esf,efd->esd/dot_general | solution.py:29
  258.1 7.8 %gather_fusion = f32[256,3584]{1,0:T(8,128)} fusion(f32[384,3584]{1,0:T(8,128)} %bitcast.35, s32[1024]{0:T(1024)S(1)} %pad_clamp_fusion), kind=kCustom, calls=%fused_computation | custom fusion | bytes 7341056 | tf_op jit(solution)/shard_map/jit(_take)/gather | solution.py:37
  265.9 4.3 %broadcast_select_fusion = f32[256,3584]{1,0:T(8,128)} fusion(f32[256,3584]{1,0:T(8,128)} %gather_fusion, pred[256]{0:T(512)(128)(4,1)S(1)} %get-tuple-element.5), kind=kLoop, calls=%fused_computation.3 | loop fusion | flops 917504 | bytes 7340288 | tf_op jit(solution)/shard_map/jit(_take)/select_n | solution.py:37
  270.2 0.0 copy-start
  270.2 0.0 reduce-scatter.2.cloned.1.call-update
  270.2 39.9 %reduce-scatter.2.cloned.1.call-done = f32[64,3584]{1,0:T(8,128)} async-done(((f32[256,3584]{1,0:T(8,128)}), f32[64,3584]{1,0:T(8,128)}) %reduce-scatter.2.cloned.1.call-update) | async-done | bytes 917520 | tf_op jit(solution)/shard_map/reduce_scatter | solution.py:38
  310.2 0.0 copy-done
  310.2 2.1 multiply_convert_fusion
  (8 shorter events, 0.1 us)
Async XLA Ops:
  6.5 26.2 %all-gather.5.cloned.1.call-start = ((), (), s32[]{:S(2)}) async-start(), calls=%async_computation.1 | async-start | bytes 2293760 | tf_op jit(solution)/shard_map/all_gather | solution.py:8
  7.3 99.2 %all-gather.7.cloned.1.call-start = ((), (), s32[]{:S(2)}) async-start(), calls=%async_computation.2 | async-start | bytes 4587520 | tf_op jit(solution)/shard_map/all_gather | solution.py:26
  8.0 170.7 %all-gather.11.cloned.1.call-start = ((), (), s32[]{:S(2)}) async-start(), calls=%async_computation.4 | async-start | bytes 4587520 | tf_op jit(solution)/shard_map/all_gather | solution.py:32
  8.7 242.1 %all-gather.9.cloned.1.call-start = ((), (), s32[]{:S(2)}) async-start(), calls=%async_computation.3 | async-start | bytes 4587520 | tf_op jit(solution)/shard_map/all_gather | solution.py:27
  9.3 300.9 %reduce-scatter.2.cloned.1.call-start = ((), (), s32[]{:S(2)}) async-start(), calls=%async_computation.5 | async-start | bytes 4587520 | tf_op jit(solution)/shard_map/reduce_scatter | solution.py:38
  270.2 40.0 %copy-start = (f32[64,1]{0,1:T(1,128)S(1)}, f32[64,1]{0,1:T(1,128)}, u32[]{:S(2)}) copy-start(f32[64,1]{0,1:T(1,128)} %param.8) | copy-start | bytes 772
Sparse Core Ops, SparseCore 0:
  8.9 23.8 all-gather.4
  34.3 72.0 all-gather.6
  108.0 70.6 all-gather.10
  180.1 70.6 all-gather.8
  270.4 39.7 reduce-scatter.1
where the time goes:
time: 319 us
  waiting for transfers between devices  268 us (84%)
  between operations  13.9 us (4%)
  matrix products  12.5 us (4%)
  local copies, waits for them, and re-layouts  10 us (3%)
  other arithmetic  7.37 us (2%)
  blocking collectives  6.38 us (2%)
    all_gather x1, waiting for transfers between devices, body(): up_sum = add_part(lax.all_gather(w_up, 'blk', axis=1, tiled=True))  72.1 us
    all_gather x1, waiting for transfers between devices, body(): gate_sum = add_part(lax.all_gather(w_gate, 'blk', axis=1, tiled=True))  71.3 us
    all_gather x1, waiting for transfers between devices, body(): lax.all_gather(w_down, 'blk', axis=2, tiled=True)  69.4 us
    reduce_scatter x1, waiting for transfers between devices, body(): lax.psum_scatter(partial_value, 'tok', scatter_dimension=0, tiled=True)  39.9 us
    all_gather x1, waiting for transfers between devices, body(): group_rows = lax.all_gather(tokens, 'tok', axis=0, tiled=True)  13.1 us
    gather x1, local copies, waits for them, and re-layouts, body(): partial_value = jnp.take(flat_rows, position, axis=0)  7.8 us
    dot_general x1, matrix products, body(): jnp.einsum('esf,efd->esd', hidden, lax.all_gather(w_down, 'blk', axis=2,...  7.24 us
  transfers between devices with their start and end apart: 5, of which 5 were waited for; matrix products, arithmetic and copies ran while one was open for 3% of the time, Pallas kernels for 0%

commit v1 on v0

--- a/solution.py
+++ b/solution.py
@@ -1,10 +1,17 @@
+import functools
+
 import jax
 import jax.numpy as jnp
 from jax import lax
+from jax.experimental import pallas as pl
+from jax.experimental.pallas import tpu as pltpu
 from jax.sharding import PartitionSpec as P
 
-
-def body(tokens, expert_ids, gate_values, w_gate, w_up, w_down):
+LANES = 128
+SUBLANES = 8
+
+
+def gathered_body(tokens, expert_ids, gate_values, w_gate, w_up, w_down):
     group_rows = lax.all_gather(tokens, "tok", axis=0, tiled=True)
     group_routes = lax.all_gather(expert_ids, "tok", axis=0, tiled=True)[:, 0]
     experts = w_gate.shape[0]
@@ -39,7 +46,255 @@
     return (gate_values * summed).astype(jnp.bfloat16)
 
 
+def kernel(
+    nb, nt, tok_hbm, meta_hbm, wg_hbm, wu_hbm, wd_hbm, out_ref,
+    tok, meta, wg, wu, wd, xs, part_own, part_send, part_recv, hid, ys, ycore, yx_send, yx_recv, fin_send,
+    local_sem, z_send, z_recv, x_send, x_recv, c_send, c_recv, f_send, f_recv, m_send, m_recv,
+    p_send, p_recv, h_send, h_recv, yc_send_sem, yc_recv_sem, yx_send_sem, yx_recv_sem, o_send, o_recv,
+):
+    g, b, t = lax.axis_index("groups"), lax.axis_index("blk"), lax.axis_index("tok")
+    rows, width = tok.shape[0], xs.shape[3]
+    experts, ff = wg.shape[0], wg.shape[2]
+    half = nt // 2
+    f32, bf16 = jnp.float32, jnp.bfloat16
+    pair = t + 1 - 2 * lax.rem(t, 2)
+
+    def blk(k):
+        return lax.rem(b + k + nb, nb)
+
+    def tk(base, j):
+        return lax.rem(base + j + nt, nt)
+
+    def cols(block):
+        return pl.ds(pl.multiple_of(block * width, LANES), width)
+
+    def remote(src, dst, send, recv, to_b, to_t):
+        copy = pltpu.make_async_remote_copy(
+            src_ref=src, dst_ref=dst, send_sem=send, recv_sem=recv,
+            device_id=(g, to_b, to_t), device_id_type=pl.DeviceIdType.MESH,
+        )
+        copy.start()
+        sends.append(copy)
+
+    def arrived(dst, recv):
+        pltpu.make_async_copy(dst, dst, recv).wait()
+
+    sends = []
+    local = [
+        pltpu.make_async_copy(tok_hbm, tok, local_sem.at[0]),
+        pltpu.make_async_copy(meta_hbm, meta.at[b, t], local_sem.at[1]),
+        pltpu.make_async_copy(tok_hbm.at[:, cols(b)], xs.at[b, t], local_sem.at[2]),
+        pltpu.make_async_copy(wg_hbm, wg, local_sem.at[3]),
+        pltpu.make_async_copy(wu_hbm, wu, local_sem.at[4]),
+        pltpu.make_async_copy(wd_hbm, wd, local_sem.at[5]),
+    ]
+    for copy in local:
+        copy.start()
+
+    barrier = pltpu.get_barrier_semaphore()
+    for k in range(nb):
+        for j in range(nt):
+            if k or j:
+                pl.semaphore_signal(
+                    barrier, inc=1, device_id=(g, blk(k), tk(t, j)),
+                    device_id_type=pl.DeviceIdType.MESH,
+                )
+    pl.semaphore_wait(barrier, nb * nt - 1)
+
+    order = [0]
+    for k in range(1, nb // 2 + 1):
+        order += [k] if 2 * k == nb else [k, nb - k]
+    others = order[1:]
+
+    local[0].wait()
+    for k in others:
+        remote(tok.at[:, cols(blk(k))], xs.at[b, t], z_send.at[k], z_recv.at[k], blk(k), t)
+    local[1].wait()
+    for k in order:
+        for j in range(nt):
+            if k or j:
+                remote(meta.at[b, t], meta.at[b, t], m_send.at[k, j], m_recv.at[k, j], blk(k), tk(t, j))
+    local[2].wait()
+
+    def spread(k):
+        source = blk(-k)
+        if k:
+            arrived(xs.at[source, t], z_recv.at[k])
+        mine = xs.at[source, t]
+        for j in range(1, half):
+            remote(mine, mine, x_send.at[k, j], x_recv.at[k, j], b, tk(t, 2 * j))
+        remote(mine, mine, c_send.at[k], c_recv.at[k], b, pair)
+
+    def pass_on(k):
+        source = blk(-k)
+        for j in range(1, half):
+            theirs = xs.at[source, tk(t, -2 * j)]
+            arrived(theirs, x_recv.at[k, j])
+            remote(theirs, theirs, f_send.at[k, j], f_recv.at[k, j], b, pair)
+
+    def column(k, row):
+        flat = meta[blk(-k)].reshape(nt * SUBLANES, LANES)
+        turned = jnp.transpose(flat)
+        return jnp.concatenate(
+            [turned[:rows, SUBLANES * i + row:SUBLANES * i + row + 1] for i in range(nt)], axis=0
+        )
+
+    def contract(k):
+        source = blk(-k)
+        arrived(xs.at[source, pair], c_recv.at[k])
+        for j in range(1, half):
+            arrived(xs.at[source, tk(pair, -2 * j)], f_recv.at[k, j])
+        for j in range(nt):
+            if k or j:
+                arrived(meta.at[source, tk(t, -j)], m_recv.at[k, j])
+        if k == 0:
+            local[3].wait()
+            local[4].wait()
+        routes = column(k, 0)
+        x = xs[source].reshape(nt * rows, width)
+        for at, weights in ((0, wg), (ff, wu)):
+            total = None
+            for e in range(experts):
+                value = jnp.dot(x, weights[e], preferred_element_type=f32)
+                total = value if e == 0 else jnp.where(routes == e, value, total)
+            if k == 0:
+                part_own[:, at:at + ff] = total
+            else:
+                part_send[k, :, at:at + ff] = total.astype(bf16)
+        if k:
+            remote(part_send.at[k], part_recv.at[k], p_send.at[k], p_recv.at[k], source, t)
+
+    stage = [(spread, 0), (pass_on, 1), (contract, 2)]
+    for step in range(nb + 2):
+        for run, lag in stage:
+            at = step - lag
+            if 0 <= at < nb:
+                run(order[at])
+
+    for k in others:
+        arrived(part_recv.at[k], p_recv.at[k])
+    gate = part_own[:, :ff]
+    up = part_own[:, ff:]
+    for k in others:
+        gate = gate + part_recv[k, :, :ff].astype(f32)
+        up = up + part_recv[k, :, ff:].astype(f32)
+    hid[b] = (gate / (1.0 + jnp.exp(-gate)) * up * column(0, 1)).astype(bf16)
+    for k in others:
+        remote(hid.at[b], hid.at[b], h_send.at[k], h_recv.at[k], blk(k), t)
+
+    def expand(k):
+        source = blk(-k)
+        if k:
+            arrived(hid.at[source], h_recv.at[k])
+        else:
+            local[5].wait()
+        routes = column(k, 0)
+        h = hid[source].astype(f32)
+        routed = jnp.concatenate(
+            [jnp.where(routes == e, h, 0.0).astype(bf16) for e in range(experts)], axis=1
+        )
+        ys[k] = jnp.dot(routed, wd[...].reshape(experts * ff, width), preferred_element_type=f32)
+        for j in reversed(range(half)):
+            remote(
+                ys.at[k, rows_of(tk(pair, 2 * j))], ycore.at[k, j],
+                yc_send_sem.at[k, j], yc_recv_sem.at[k, j], b, pair,
+            )
+
+    def rows_of(index):
+        return pl.ds(pl.multiple_of(index * rows, SUBLANES), rows)
+
+    def exchange(k):
+        for j in range(1, half):
+            arrived(ycore.at[k, j], yc_recv_sem.at[k, j])
+            total = ys[k, rows_of(tk(t, 2 * j)), :] + ycore[k, j]
+            yx_send[k, j] = total.astype(bf16)
+            remote(
+                yx_send.at[k, j], yx_recv.at[k, j],
+                yx_send_sem.at[k, j], yx_recv_sem.at[k, j], b, tk(t, 2 * j),
+            )
+
+    def finish(k):
+        arrived(ycore.at[k, 0], yc_recv_sem.at[k, 0])
+        total = ys[k, rows_of(t), :] + ycore[k, 0]
+        for j in range(1, half):
+            arrived(yx_recv.at[k, j], yx_recv_sem.at[k, j])
+            total = total + yx_recv[k, j].astype(f32)
+        if k:
+            fin_send[k] = total.astype(bf16)
+            remote(fin_send.at[k], out_ref.at[:, cols(b)], o_send.at[k], o_recv.at[k], blk(-k), t)
+        else:
+            out_ref[:, cols(b)] = total.astype(bf16)
+
+    stage = [(expand, 0), (exchange, 1), (finish, 2)]
+    for step in range(nb + 2):
+        for run, lag in stage:
+            at = step - lag
+            if 0 <= at < nb:
+                run(order[at])
+
+    for k in others:
+        arrived(out_ref.at[:, cols(blk(k))], o_recv.at[k])
+    for copy in sends:
+        copy.wait_send()
+
+
+def stationary_body(nb, nt, tokens, expert_ids, gate_values, w_gate, w_up, w_down):
+    rows, features = tokens.shape
+    experts, width, ff = w_gate.shape
+    f32, bf16 = jnp.float32, jnp.bfloat16
+    lines = jnp.stack([expert_ids[:, 0].astype(f32), gate_values[:, 0]])
+    meta = jnp.pad(lines, ((0, SUBLANES - 2), (0, LANES - rows)))
+    block, half = nt * rows, nt // 2
+    dma = pltpu.SemaphoreType.DMA
+    anywhere = pl.BlockSpec(memory_space=pl.ANY)
+    return pl.pallas_call(
+        functools.partial(kernel, nb, nt),
+        out_shape=jax.ShapeDtypeStruct((rows, features), bf16),
+        in_specs=[anywhere] * 5,
+        out_specs=pl.BlockSpec(memory_space=pltpu.VMEM),
+        scratch_shapes=[
+            pltpu.VMEM((rows, features), bf16),
+            pltpu.VMEM((nb, nt, SUBLANES, LANES), f32),
+            pltpu.VMEM(w_gate.shape, bf16),
+            pltpu.VMEM(w_up.shape, bf16),
+            pltpu.VMEM(w_down.shape, bf16),
+            pltpu.VMEM((nb, nt, rows, width), bf16),
+            pltpu.VMEM((block, 2 * ff), f32),
+            pltpu.VMEM((nb, block, 2 * ff), bf16),
+            pltpu.VMEM((nb, block, 2 * ff), bf16),
+            pltpu.VMEM((nb, block, ff), bf16),
+            pltpu.VMEM((nb, block, width), f32),
+            pltpu.VMEM((nb, half, rows, width), f32),
+            pltpu.VMEM((nb, half, rows, width), bf16),
+            pltpu.VMEM((nb, half, rows, width), bf16),
+            pltpu.VMEM((nb, rows, width), bf16),
+            dma((6,)),
+            dma((nb,)), dma((nb,)),
+            dma((nb, half)), dma((nb, half)),
+            dma((nb,)), dma((nb,)),
+            dma((nb, half)), dma((nb, half)),
+            dma((nb, nt)), dma((nb, nt)),
+            dma((nb,)), dma((nb,)),
+            dma((nb,)), dma((nb,)),
+            dma((nb, half)), dma((nb, half)),
+            dma((nb, half)), dma((nb, half)),
+            dma((nb,)), dma((nb,)),
+        ],
+        compiler_params=pltpu.CompilerParams(collective_id=0, has_side_effects=True),
+    )(tokens, meta, w_gate, w_up, w_down)
+
+
 def solution(mesh):
+    nb, nt = mesh.shape["blk"], mesh.shape["tok"]
+
+    def body(tokens, expert_ids, gate_values, w_gate, w_up, w_down):
+        rows = tokens.shape[0]
+        width, ff = w_gate.shape[1], w_gate.shape[2]
+        fits = width % LANES == 0 and ff % LANES == 0 and rows % 16 == 0 and rows <= LANES
+        if fits and nt % 2 == 0 and nb <= 8:
+            return stationary_body(nb, nt, tokens, expert_ids, gate_values, w_gate, w_up, w_down)
+        return gathered_body(tokens, expert_ids, gate_values, w_gate, w_up, w_down)
+
     return jax.shard_map(
         body,
         mesh=mesh,

time: 319 us -> 77.1 us (0.24)
  waiting for transfers between devices: 268 us -> 0 us
  Pallas kernels: 0 us -> 73.2 us
  between operations: 13.9 us -> 0.01 us
  matrix products: 12.5 us -> 0 us
  local copies, waits for them, and re-layouts: 10 us -> 3.12 us
  other arithmetic: 7.37 us -> 0.6 us
  blocking collectives: 6.38 us -> 0 us
    all_gather x4 -> x0, waiting for transfers between devices: 226 us -> none  [the longest x1 72.1 us: body(): up_sum = add_part(lax.all_gather(w_up, 'blk', axis=1, tiled=True))]
    pallas_call x0 -> x1, Pallas kernels: none -> 73.2 us  [stationary_body(): pl.pallas_call(functools.partial(kernel, nb, nt), out_shape=jax.ShapeDtyp...]
    reduce_scatter x1 -> x0, waiting for transfers between devices: 39.9 us -> none  [body(): lax.psum_scatter(partial_value, 'tok', scatter_dimension=0, tiled=True)]
    dot_general x3 -> x0, matrix products: 12.5 us -> none  [the longest x1 7.24 us: body(): jnp.einsum('esf,efd->esd', hidden, lax.all_gather(w_down, 'blk', axis=2,...]
    gather x1 -> x0, local copies, waits for them, and re-layouts: 7.8 us -> none  [body(): partial_value = jnp.take(flat_rows, position, axis=0)]
    eq x1 -> x0, blocking collectives: 6.38 us -> none  [body(): onehot = (group_routes[:, None] == expert_range[None, :]).astype(jnp.int32)]
    select_n x1 -> x0, other arithmetic: 4.34 us -> none  [body(): partial_value = jnp.take(flat_rows, position, axis=0)]
  transfers between devices with their start and end apart: 5 -> 0, of which waited for: 5 -> 0; matrix products, arithmetic and copies ran while one was open for 3% -> 0% of each run, Pallas kernels for 0% -> 0%
where the time goes in v1:
time: 77.1 us; the launch traced here: 76.9 us
  Pallas kernels  73.2 us (95%)
  local copies, waits for them, and re-layouts  3.12 us (4%)
    pallas_call x1, Pallas kernels, stationary_body(): pl.pallas_call(functools.partial(kernel, nb, nt), out_shape=jax.ShapeDtyp...  73.2 us
    unnamed x5, local copies, waits for them, and re-layouts  3.12 us

profile of v1, /device:TPU:0, one launch (start us, length us, event | category | flops | bytes accessed | tf_op | source)
XLA Modules:
  0.0 76.9 jit_solution(12292621701757021292)
XLA Ops:
  0.0 0.0 copy-start.1
  0.0 0.7 copy-done.1
  0.7 0.0 copy-start
  0.7 0.7 copy-done
  1.3 0.6 select_maximum_fusion.meta_hbm
  1.9 73.2 %shard_map.64 = bf16[64,3584]{1,0:T(8,128)(2,1)} custom-call(bf16[64,3584]{1,0:T(8,128)(2,1)} %tok_hbm.1, f32[8,128]{1,0:T(8,128)} %select_maximum_fusion.meta_hbm, bf16[2,896,256]{2,1,0:T(8,128)(2,1)} %wg_hbm.1, bf16[2,896,256]{2,1,0:T(8,128)(2,1)} %wu_hbm.1, bf16[2,256,896]{2,1,0:T(8,128)(2,1)} %wd_hbm.1), custom_call_target="tpu_custom_call" | custom-call | tf_op jit(solution)/shard_map/pallas_call | solution.py:250
  75.1 1.8 %copy.8 = bf16[64,3584]{1,0:T(8,128)(2,1)} copy(bf16[64,3584]{1,0:T(8,128)(2,1)} %shard_map.64) | data formatting | bytes 917504
  (1 shorter events, 0.0 us)
Async XLA Ops:
  0.0 0.7 copy-start.1
  0.7 0.7 copy-start

commit v2 on v1

--- a/solution.py
+++ b/solution.py
@@ -9,6 +9,7 @@
 
 LANES = 128
 SUBLANES = 8
+CHUNKS = 2
 
 
 def gathered_body(tokens, expert_ids, gate_values, w_gate, w_up, w_down):
@@ -47,8 +48,8 @@
 
 
 def kernel(
-    nb, nt, tok_hbm, meta_hbm, wg_hbm, wu_hbm, wd_hbm, out_ref,
-    tok, meta, wg, wu, wd, xs, part_own, part_send, part_recv, hid, ys, ycore, yx_send, yx_recv, fin_send,
+    nb, nt, tok_hbm, ids_ref, values_ref, wg_hbm, wu_hbm, wd_hbm, out_ref,
+    tok, meta, wg, wu, wd, xs, part, part_send, part_recv, hid, ys, ycore, yx_send, yx_recv, fin_send,
     local_sem, z_send, z_recv, x_send, x_recv, c_send, c_recv, f_send, f_recv, m_send, m_recv,
     p_send, p_recv, h_send, h_recv, yc_send_sem, yc_recv_sem, yx_send_sem, yx_recv_sem, o_send, o_recv,
 ):
@@ -59,8 +60,17 @@
     f32, bf16 = jnp.float32, jnp.bfloat16
     pair = t + 1 - 2 * lax.rem(t, 2)
 
+    outer = lax.rem((b + 1) // 2 + 1, 2)
+    piece = nt * rows // CHUNKS
+
     def blk(k):
-        return lax.rem(b + k + nb, nb)
+        low, high = lax.rem(b, 2), b // 2
+        low = 1 - low if k % 2 else low
+        high = 1 - high if k // 2 else high
+        return 2 * high + low
+
+    def chunk(c):
+        return pl.ds(c * piece, piece)
 
     def tk(base, j):
         return lax.rem(base + j + nt, nt)
@@ -82,14 +92,17 @@
     sends = []
     local = [
         pltpu.make_async_copy(tok_hbm, tok, local_sem.at[0]),
-        pltpu.make_async_copy(meta_hbm, meta.at[b, t], local_sem.at[1]),
-        pltpu.make_async_copy(tok_hbm.at[:, cols(b)], xs.at[b, t], local_sem.at[2]),
+        pltpu.make_async_copy(tok_hbm.at[:, cols(b)], xs.at[b, t], local_sem.at[1]),
+        pltpu.make_async_copy(wd_hbm, wd, local_sem.at[2]),
         pltpu.make_async_copy(wg_hbm, wg, local_sem.at[3]),
         pltpu.make_async_copy(wu_hbm, wu, local_sem.at[4]),
-        pltpu.make_async_copy(wd_hbm, wd, local_sem.at[5]),
     ]
     for copy in local:
         copy.start()
+
+    meta[b, t] = jnp.zeros((SUBLANES, LANES), f32)
+    meta[b, t, 0:1, :rows] = ids_ref[...].astype(f32)
+    meta[b, t, 1:2, :rows] = values_ref[...]
 
     barrier = pltpu.get_barrier_semaphore()
     for k in range(nb):
@@ -101,23 +114,20 @@
                 )
     pl.semaphore_wait(barrier, nb * nt - 1)
 
-    order = [0]
-    for k in range(1, nb // 2 + 1):
-        order += [k] if 2 * k == nb else [k, nb - k]
+    order = list(range(nb))
     others = order[1:]
 
     local[0].wait()
     for k in others:
         remote(tok.at[:, cols(blk(k))], xs.at[b, t], z_send.at[k], z_recv.at[k], blk(k), t)
-    local[1].wait()
     for k in order:
         for j in range(nt):
             if k or j:
                 remote(meta.at[b, t], meta.at[b, t], m_send.at[k, j], m_recv.at[k, j], blk(k), tk(t, j))
-    local[2].wait()
+    local[1].wait()
 
     def spread(k):
-        source = blk(-k)
+        source = blk(k)
         if k:
             arrived(xs.at[source, t], z_recv.at[k])
         mine = xs.at[source, t]
@@ -126,21 +136,21 @@
         remote(mine, mine, c_send.at[k], c_recv.at[k], b, pair)
 
     def pass_on(k):
-        source = blk(-k)
+        source = blk(k)
         for j in range(1, half):
             theirs = xs.at[source, tk(t, -2 * j)]
             arrived(theirs, x_recv.at[k, j])
             remote(theirs, theirs, f_send.at[k, j], f_recv.at[k, j], b, pair)
 
     def column(k, row):
-        flat = meta[blk(-k)].reshape(nt * SUBLANES, LANES)
+        flat = meta[blk(k)].reshape(nt * SUBLANES, LANES)
         turned = jnp.transpose(flat)
         return jnp.concatenate(
             [turned[:rows, SUBLANES * i + row:SUBLANES * i + row + 1] for i in range(nt)], axis=0
         )
 
     def contract(k):
-        source = blk(-k)
+        source = blk(k)
         arrived(xs.at[source, pair], c_recv.at[k])
         for j in range(1, half):
             arrived(xs.at[source, tk(pair, -2 * j)], f_recv.at[k, j])
@@ -157,12 +167,33 @@
             for e in range(experts):
                 value = jnp.dot(x, weights[e], preferred_element_type=f32)
                 total = value if e == 0 else jnp.where(routes == e, value, total)
-            if k == 0:
-                part_own[:, at:at + ff] = total
-            else:
-                part_send[k, :, at:at + ff] = total.astype(bf16)
-        if k:
-            remote(part_send.at[k], part_recv.at[k], p_send.at[k], p_recv.at[k], source, t)
+            part[k, :, at:at + ff] = total
+        if k == 1:
+            part_send[k] = part[k].astype(bf16)
+            for c in range(CHUNKS):
+                send_part(k, c).start()
+        elif k:
+            @pl.when(outer == 1)
+            def _():
+                part_send[k] = part[k].astype(bf16)
+                for c in range(CHUNKS):
+                    send_part(k, c).start()
+
+    def send_part(k, c):
+        slot = 0 if k == 1 else outer * (5 - k) + 1 - outer
+        target = blk(1) if k == 1 else outer * blk(1) + (1 - outer) * blk(k)
+        return pltpu.make_async_remote_copy(
+            src_ref=part_send.at[k, chunk(c)], dst_ref=part_recv.at[slot, chunk(c)],
+            send_sem=p_send.at[k, c], recv_sem=p_recv.at[slot, c],
+            device_id=(g, target, t), device_id_type=pl.DeviceIdType.MESH,
+        )
+
+    def relay(k, c):
+        @pl.when(outer == 0)
+        def _():
+            arrived(part_recv.at[k, chunk(c)], p_recv.at[k, c])
+            part_send[k, chunk(c), :] = (part[k, chunk(c), :] + part_recv[k, chunk(c), :].astype(f32)).astype(bf16)
+            send_part(k, c).start()
 
     stage = [(spread, 0), (pass_on, 1), (contract, 2)]
     for step in range(nb + 2):
@@ -171,23 +202,38 @@
             if 0 <= at < nb:
                 run(order[at])
 
-    for k in others:
-        arrived(part_recv.at[k], p_recv.at[k])
-    gate = part_own[:, :ff]
-    up = part_own[:, ff:]
-    for k in others:
-        gate = gate + part_recv[k, :, :ff].astype(f32)
-        up = up + part_recv[k, :, ff:].astype(f32)
-    hid[b] = (gate / (1.0 + jnp.exp(-gate)) * up * column(0, 1)).astype(bf16)
-    for k in others:
-        remote(hid.at[b], hid.at[b], h_send.at[k], h_recv.at[k], blk(k), t)
+    for k in (3, 2):
+        for c in range(CHUNKS):
+            relay(k, c)
+
+    values = column(0, 1)
+    for c in range(CHUNKS):
+        total = part[0, chunk(c), :]
+        for slot in (0, 1):
+            arrived(part_recv.at[slot, chunk(c)], p_recv.at[slot, c])
+            total = total + part_recv[slot, chunk(c), :].astype(f32)
+        gate, up = total[:, :ff], total[:, ff:]
+        scale = values[c * piece:(c + 1) * piece]
+        hid[b, chunk(c), :] = (gate / (1.0 + jnp.exp(-gate)) * up * scale).astype(bf16)
+        for k in (2, 1):
+            mine = hid.at[b, chunk(c)]
+            remote(mine, mine, h_send.at[k, c], h_recv.at[k, c], blk(k), t)
+
+    def forward(c):
+        theirs = hid.at[blk(2), chunk(c)]
+        arrived(theirs, h_recv.at[2, c])
+        remote(theirs, theirs, h_send.at[3, c], h_recv.at[3, c], blk(1), t)
 
     def expand(k):
-        source = blk(-k)
-        if k:
-            arrived(hid.at[source], h_recv.at[k])
-        else:
-            local[5].wait()
+        source = blk(k)
+        if k == 0:
+            local[2].wait()
+        elif k != 2:
+            for c in range(CHUNKS):
+                arrived(hid.at[source, chunk(c)], h_recv.at[k, c])
+        if k == 1:
+            for c in range(CHUNKS):
+                forward(c)
         routes = column(k, 0)
         h = hid[source].astype(f32)
         routed = jnp.concatenate(
@@ -221,7 +267,7 @@
             total = total + yx_recv[k, j].astype(f32)
         if k:
             fin_send[k] = total.astype(bf16)
-            remote(fin_send.at[k], out_ref.at[:, cols(b)], o_send.at[k], o_recv.at[k], blk(-k), t)
+            remote(fin_send.at[k], out_ref.at[:, cols(b)], o_send.at[k], o_recv.at[k], blk(k), t)
         else:
             out_ref[:, cols(b)] = total.astype(bf16)
 
@@ -236,22 +282,24 @@
         arrived(out_ref.at[:, cols(blk(k))], o_recv.at[k])
     for copy in sends:
         copy.wait_send()
+    for k in others:
+        for c in range(CHUNKS):
+            send_part(k, c).wait_send()
 
 
 def stationary_body(nb, nt, tokens, expert_ids, gate_values, w_gate, w_up, w_down):
     rows, features = tokens.shape
     experts, width, ff = w_gate.shape
     f32, bf16 = jnp.float32, jnp.bfloat16
-    lines = jnp.stack([expert_ids[:, 0].astype(f32), gate_values[:, 0]])
-    meta = jnp.pad(lines, ((0, SUBLANES - 2), (0, LANES - rows)))
     block, half = nt * rows, nt // 2
     dma = pltpu.SemaphoreType.DMA
+    vmem = pl.BlockSpec(memory_space=pltpu.VMEM)
     anywhere = pl.BlockSpec(memory_space=pl.ANY)
     return pl.pallas_call(
         functools.partial(kernel, nb, nt),
         out_shape=jax.ShapeDtypeStruct((rows, features), bf16),
-        in_specs=[anywhere] * 5,
-        out_specs=pl.BlockSpec(memory_space=pltpu.VMEM),
+        in_specs=[anywhere, vmem, vmem, anywhere, anywhere, anywhere],
+        out_specs=vmem,
         scratch_shapes=[
             pltpu.VMEM((rows, features), bf16),
             pltpu.VMEM((nb, nt, SUBLANES, LANES), f32),
@@ -259,7 +307,7 @@
             pltpu.VMEM(w_up.shape, bf16),
             pltpu.VMEM(w_down.shape, bf16),
             pltpu.VMEM((nb, nt, rows, width), bf16),
-            pltpu.VMEM((block, 2 * ff), f32),
+            pltpu.VMEM((nb, block, 2 * ff), f32),
             pltpu.VMEM((nb, block, 2 * ff), bf16),
             pltpu.VMEM((nb, block, 2 * ff), bf16),
             pltpu.VMEM((nb, block, ff), bf16),
@@ -268,20 +316,20 @@
             pltpu.VMEM((nb, half, rows, width), bf16),
             pltpu.VMEM((nb, half, rows, width), bf16),
             pltpu.VMEM((nb, rows, width), bf16),
-            dma((6,)),
+            dma((5,)),
             dma((nb,)), dma((nb,)),
             dma((nb, half)), dma((nb, half)),
             dma((nb,)), dma((nb,)),
             dma((nb, half)), dma((nb, half)),
             dma((nb, nt)), dma((nb, nt)),
-            dma((nb,)), dma((nb,)),
-            dma((nb,)), dma((nb,)),
+            dma((nb, CHUNKS)), dma((nb, CHUNKS)),
+            dma((nb, CHUNKS)), dma((nb, CHUNKS)),
             dma((nb, half)), dma((nb, half)),
             dma((nb, half)), dma((nb, half)),
             dma((nb,)), dma((nb,)),
         ],
         compiler_params=pltpu.CompilerParams(collective_id=0, has_side_effects=True),
-    )(tokens, meta, w_gate, w_up, w_down)
+    )(tokens, expert_ids.reshape(1, rows), gate_values.reshape(1, rows), w_gate, w_up, w_down)
 
 
 def solution(mesh):
@@ -291,7 +339,7 @@
         rows = tokens.shape[0]
         width, ff = w_gate.shape[1], w_gate.shape[2]
         fits = width % LANES == 0 and ff % LANES == 0 and rows % 16 == 0 and rows <= LANES
-        if fits and nt % 2 == 0 and nb <= 8:
+        if fits and nt % 2 == 0 and nb == 4 and nt * rows % (16 * CHUNKS) == 0:
             return stationary_body(nb, nt, tokens, expert_ids, gate_values, w_gate, w_up, w_down)
         return gathered_body(tokens, expert_ids, gate_values, w_gate, w_up, w_down)
 

time: 77.1 us -> 74.1 us (0.961)
  local copies, waits for them, and re-layouts: 3.12 us -> 1.82 us
  Pallas kernels: 73.2 us -> 72.1 us
    unnamed x5 -> x1, local copies, waits for them, and re-layouts: 3.12 us -> 1.82 us
    pallas_call x1, Pallas kernels: 73.2 us -> 72.1 us  [stationary_body(): pl.pallas_call(functools.partial(kernel, nb, nt), out_shape=jax.ShapeDtyp...]
where the time goes in v2:
time: 74.1 us; the launch traced here: 73.9 us
  Pallas kernels  72.1 us (97%)
  local copies, waits for them, and re-layouts  1.82 us (2%)
    pallas_call x1, Pallas kernels, stationary_body(): pl.pallas_call(functools.partial(kernel, nb, nt), out_shape=jax.ShapeDtyp...  72.1 us
    unnamed x1, local copies, waits for them, and re-layouts  1.82 us

profile of v2, /device:TPU:0, one launch (start us, length us, event | category | flops | bytes accessed | tf_op | source)
XLA Modules:
  0.0 73.9 jit_solution(17886294387569012408)
XLA Ops:
  0.0 72.1 %shard_map.64 = bf16[64,3584]{1,0:T(8,128)(2,1)} custom-call(bf16[64,3584]{1,0:T(8,128)(2,1)} %tok_hbm.1, s32[1,64]{1,0:T(1,128)} %bitcast.2, f32[1,64]{1,0:T(1,128)} %bitcast.3, bf16[2,896,256]{2,1,0:T(8,128)(2,1)} %wg_hbm.1, bf16[2,896,256]{2,1,0:T(8,128)(2,1)} %wu_hbm.1, bf16[2,256,896]{2,1,0:T(8,128)(2,1)} %wd_hbm.1), custom_call_target="tpu_custom_call" | custom-call | tf_op jit(solution)/shard_map/pallas_call | solution.py:298
  72.1 1.8 %copy.8 = bf16[64,3584]{1,0:T(8,128)(2,1)} copy(bf16[64,3584]{1,0:T(8,128)(2,1)} %shard_map.64) | data formatting | bytes 917504

commit v3 on v2

v3 whole, which is shorter than its diff:
```python
import functools

import jax
import jax.numpy as jnp
from jax import lax
from jax.experimental import pallas as pl
from jax.experimental.pallas import tpu as pltpu
from jax.sharding import PartitionSpec as P

LANES = 128
SUBLANES = 8
CHUNKS = 1
WAVES = 2


def gathered_body(tokens, expert_ids, gate_values, w_gate, w_up, w_down):
    group_rows = lax.all_gather(tokens, "tok", axis=0, tiled=True)
    group_routes = lax.all_gather(expert_ids, "tok", axis=0, tiled=True)[:, 0]
    experts = w_gate.shape[0]
    count_rows = group_rows.shape[0]
    capacity = 3 * count_rows // 4
    expert_range = jnp.arange(experts, dtype=jnp.int32)
    onehot = (group_routes[:, None] == expert_range[None, :]).astype(jnp.int32)
    slot_rank = jnp.sum((jnp.cumsum(onehot, axis=0) - onehot) * onehot, axis=1)
    expert_match = group_routes[None, None, :] == expert_range[:, None, None]
    slot_match = slot_rank[None, None, :] == jnp.arange(capacity, dtype=jnp.int32)[None, :, None]
    dispatch = (expert_match & slot_match).astype(jnp.bfloat16)
    slots = jnp.einsum(
        "esg,gd->esd", dispatch, group_rows, preferred_element_type=jnp.float32
    ).astype(jnp.bfloat16)

    def add_part(weights):
        return jnp.einsum("esd,edf->esf", slots, weights, preferred_element_type=jnp.float32)

    gate_sum = add_part(lax.all_gather(w_gate, "blk", axis=1, tiled=True))
    up_sum = add_part(lax.all_gather(w_up, "blk", axis=1, tiled=True))
    hidden = (jax.nn.silu(gate_sum) * up_sum).astype(jnp.bfloat16)
    slot_out = jnp.einsum(
        "esf,efd->esd",
        hidden,
        lax.all_gather(w_down, "blk", axis=2, tiled=True),
        preferred_element_type=jnp.float32,
    )
    flat_rows = slot_out.reshape(experts * capacity, slot_out.shape[2])
    position = group_routes * capacity + slot_rank
    partial_value = jnp.take(flat_rows, position, axis=0)
    summed = lax.psum_scatter(partial_value, "tok", scatter_dimension=0, tiled=True)
    return (gate_values * summed).astype(jnp.bfloat16)


def kernel(
    nb, nt, tok_hbm, ids_ref, values_ref, wg_hbm, wu_hbm, wd_hbm, out_ref,
    tok, meta, wg, wu, wd, xs, part, part_send, part_recv, hid, ys, ycore, yx_send, yx_recv, fin_send,
    local_sem, z_send, z_recv, x_send, x_recv, c_send, c_recv, f_send, f_recv, m_send, m_recv,
    p_send, p_recv, h_send, h_recv, yc_send_sem, yc_recv_sem, yx_send_sem, yx_recv_sem, o_send, o_recv,
):
    g, b, t = lax.axis_index("groups"), lax.axis_index("blk"), lax.axis_index("tok")
    all_rows, width = tok.shape[0], xs.shape[4]
    rows = all_rows // WAVES
    experts, ff = wg.shape[0], wg.shape[2]
    half = nt // 2
    f32, bf16 = jnp.float32, jnp.bfloat16
    pair = t + 1 - 2 * lax.rem(t, 2)

    outer = lax.rem((b + 1) // 2 + 1, 2)
    piece = nt * rows // CHUNKS

    def blk(k):
        low, high = lax.rem(b, 2), b // 2
        low = 1 - low if k % 2 else low
        high = 1 - high if k // 2 else high
        return 2 * high + low

    def chunk(c):
        return pl.ds(c * piece, piece)

    def tk(base, j):
        return lax.rem(base + j + nt, nt)

    def cols(block):
        return pl.ds(pl.multiple_of(block * width, LANES), width)

    def remote(src, dst, send, recv, to_b, to_t):
        copy = pltpu.make_async_remote_copy(
            src_ref=src, dst_ref=dst, send_sem=send, recv_sem=recv,
            device_id=(g, to_b, to_t), device_id_type=pl.DeviceIdType.MESH,
        )
        copy.start()
        sends.append(copy)

    def arrived(dst, recv):
        pltpu.make_async_copy(dst, dst, recv).wait()

    sends = []
    own = [
        pltpu.make_async_copy(tok_hbm.at[pl.ds(w * rows, rows), cols(b)], xs.at[w, b, t], local_sem.at[5 + w])
        for w in range(WAVES)
    ]
    local = [
        pltpu.make_async_copy(tok_hbm, tok, local_sem.at[0]),
        None,
        pltpu.make_async_copy(wd_hbm, wd, local_sem.at[2]),
        pltpu.make_async_copy(wg_hbm, wg, local_sem.at[3]),
        pltpu.make_async_copy(wu_hbm, wu, local_sem.at[4]),
    ]
    for copy in own + local:
        if copy is not None:
            copy.start()

    meta[b, t] = jnp.zeros((SUBLANES, LANES), f32)
    meta[b, t, 0:1, :all_rows] = ids_ref[...].astype(f32)
    meta[b, t, 1:2, :all_rows] = values_ref[...]

    barrier = pltpu.get_barrier_semaphore()
    for k in range(nb):
        for j in range(nt):
            if k or j:
                pl.semaphore_signal(
                    barrier, inc=1, device_id=(g, blk(k), tk(t, j)),
                    device_id_type=pl.DeviceIdType.MESH,
                )
    pl.semaphore_wait(barrier, nb * nt - 1)

    order = list(range(nb))
    others = order[1:]

    local[0].wait()
    for k in others:
        remote(tok.at[pl.ds(0, rows), cols(blk(k))], xs.at[0, b, t], z_send.at[0, k], z_recv.at[0, k], blk(k), t)
    for k in order:
        for j in range(nt):
            if k or j:
                remote(meta.at[b, t], meta.at[b, t], m_send.at[k, j], m_recv.at[k, j], blk(k), tk(t, j))
    for w in range(1, WAVES):
        for k in others:
            remote(
                tok.at[pl.ds(w * rows, rows), cols(blk(k))], xs.at[w, b, t],
                z_send.at[w, k], z_recv.at[w, k], blk(k), t,
            )
    for copy in own:
        copy.wait()

    def spread(w, k):
        source = blk(k)
        if k:
            arrived(xs.at[w, source, t], z_recv.at[w, k])
        mine = xs.at[w, source, t]
        for j in range(1, half):
            remote(mine, mine, x_send.at[w, k, j], x_recv.at[w, k, j], b, tk(t, 2 * j))
        remote(mine, mine, c_send.at[w, k], c_recv.at[w, k], b, pair)

    def pass_on(w, k):
        source = blk(k)
        for j in range(1, half):
            theirs = xs.at[w, source, tk(t, -2 * j)]
            arrived(theirs, x_recv.at[w, k, j])
            remote(theirs, theirs, f_send.at[w, k, j], f_recv.at[w, k, j], b, pair)

    def column(w, k, row):
        flat = meta[blk(k)].reshape(nt * SUBLANES, LANES)
        turned = jnp.transpose(flat)
        return jnp.concatenate(
            [turned[w * rows:(w + 1) * rows, SUBLANES * i + row:SUBLANES * i + row + 1] for i in range(nt)], axis=0
        )

    def contract(w, k):
        source = blk(k)
        arrived(xs.at[w, source, pair], c_recv.at[w, k])
        for j in range(1, half):
            arrived(xs.at[w, source, tk(pair, -2 * j)], f_recv.at[w, k, j])
        for j in range(nt):
            if w == 0 and (k or j):
                arrived(meta.at[source, tk(t, -j)], m_recv.at[k, j])
        if k == 0 and w == 0:
            local[3].wait()
            local[4].wait()
        routes = column(w, k, 0)
        x = xs[w, source].reshape(nt * rows, width)
        for at, weights in ((0, wg), (ff, wu)):
            total = None
            for e in range(experts):
                value = jnp.dot(x, weights[e], preferred_element_type=f32)
                total = value if e == 0 else jnp.where(routes == e, value, total)
            part[w, k, :, at:at + ff] = total
        if k == 1:
            part_send[w, k] = part[w, k].astype(bf16)
            for c in range(CHUNKS):
                send_part(w, k, c).start()
        elif k:
            @pl.when(outer == 1)
            def _():
                part_send[w, k] = part[w, k].astype(bf16)
                for c in range(CHUNKS):
                    send_part(w, k, c).start()

    def send_part(w, k, c):
        slot = 0 if k == 1 else outer * (5 - k) + 1 - outer
        target = blk(1) if k == 1 else outer * blk(1) + (1 - outer) * blk(k)
        return pltpu.make_async_remote_copy(
            src_ref=part_send.at[w, k, chunk(c)], dst_ref=part_recv.at[w, slot, chunk(c)],
            send_sem=p_send.at[w, k, c], recv_sem=p_recv.at[w, slot, c],
            device_id=(g, target, t), device_id_type=pl.DeviceIdType.MESH,
        )

    def relay(w, k, c):
        @pl.when(outer == 0)
        def _():
            arrived(part_recv.at[w, k, chunk(c)], p_recv.at[w, k, c])
            part_send[w, k, chunk(c), :] = (part[w, k, chunk(c), :] + part_recv[w, k, chunk(c), :].astype(f32)).astype(bf16)
            send_part(w, k, c).start()

    def activate(w):
        values = column(w, 0, 1)
        for c in range(CHUNKS):
            total = part[w, 0, chunk(c), :]
            for slot in (0, 1):
                arrived(part_recv.at[w, slot, chunk(c)], p_recv.at[w, slot, c])
                total = total + part_recv[w, slot, chunk(c), :].astype(f32)
            gate, up = total[:, :ff], total[:, ff:]
            scale = values[c * piece:(c + 1) * piece]
            hid[w, b, chunk(c), :] = (gate / (1.0 + jnp.exp(-gate)) * up * scale).astype(bf16)
            for k in (2, 1):
                mine = hid.at[w, b, chunk(c)]
                remote(mine, mine, h_send.at[w, k, c], h_recv.at[w, k, c], blk(k), t)

    def forward(w, c):
        theirs = hid.at[w, blk(2), chunk(c)]
        arrived(theirs, h_recv.at[w, 2, c])
        remote(theirs, theirs, h_send.at[w, 3, c], h_recv.at[w, 3, c], blk(1), t)

    def expand(w, k):
        source = blk(k)
        if k == 0 and w == 0:
            local[2].wait()
        if k % 2:
            for c in range(CHUNKS):
                arrived(hid.at[w, source, chunk(c)], h_recv.at[w, k, c])
        if k == 1:
            for c in range(CHUNKS):
                forward(w, c)
        routes = column(w, k, 0)
        h = hid[w, source].astype(f32)
        routed = jnp.concatenate(
            [jnp.where(routes == e, h, 0.0).astype(bf16) for e in range(experts)], axis=1
        )
        ys[w, k] = jnp.dot(routed, wd[...].reshape(experts * ff, width), preferred_element_type=f32)
        for j in reversed(range(half)):
            remote(
                ys.at[w, k, rows_of(tk(pair, 2 * j))], ycore.at[w, k, j],
                yc_send_sem.at[w, k, j], yc_recv_sem.at[w, k, j], b, pair,
            )

    def rows_of(index):
        return pl.ds(pl.multiple_of(index * rows, SUBLANES), rows)

    def exchange(w, k):
        for j in range(1, half):
            arrived(ycore.at[w, k, j], yc_recv_sem.at[w, k, j])
            total = ys[w, k, rows_of(tk(t, 2 * j)), :] + ycore[w, k, j]
            yx_send[w, k, j] = total.astype(bf16)
            remote(
                yx_send.at[w, k, j], yx_recv.at[w, k, j],
                yx_send_sem.at[w, k, j], yx_recv_sem.at[w, k, j], b, tk(t, 2 * j),
            )

    def finish(w, k):
        arrived(ycore.at[w, k, 0], yc_recv_sem.at[w, k, 0])
        total = ys[w, k, rows_of(t), :] + ycore[w, k, 0]
        for j in range(1, half):
            arrived(yx_recv.at[w, k, j], yx_recv_sem.at[w, k, j])
            total = total + yx_recv[w, k, j].astype(f32)
        if k:
            fin_send[w, k] = total.astype(bf16)
            remote(fin_send.at[w, k], out_ref.at[pl.ds(w * rows, rows), cols(b)], o_send.at[w, k], o_recv.at[w, k], blk(k), t)
        else:
            out_ref[pl.ds(w * rows, rows), cols(b)] = total.astype(bf16)


    def pipeline(w, stage, fill=()):
        fill = list(fill)
        for step in range(nb + 2):
            for run, lag in stage:
                if 0 <= step - lag < nb:
                    run(w, order[step - lag])
            if fill and step >= 2:
                fill.pop(0)()
        for rest in fill:
            rest()

    def relay_block(w, k):
        for c in range(CHUNKS):
            relay(w, k, c)

    inward = [(spread, 0), (pass_on, 1), (contract, 2)]
    outward = [(expand, 0), (exchange, 1), (finish, 2)]
    for w in range(WAVES):
        fill = []
        if w:
            fill = [functools.partial(relay_block, w - 1, k) for k in (3, 2)]
            fill += [functools.partial(activate, w - 1)]
        pipeline(w, inward, fill)
    for k in (3, 2):
        relay_block(WAVES - 1, k)
    for w in range(WAVES):
        pipeline(w, outward, [functools.partial(activate, WAVES - 1)] if w == 0 else ())

    for w in range(WAVES):
        for k in others:
            arrived(out_ref.at[pl.ds(w * rows, rows), cols(blk(k))], o_recv.at[w, k])
    for copy in sends:
        copy.wait_send()
    for w in range(WAVES):
        for k in others:
            for c in range(CHUNKS):
                send_part(w, k, c).wait_send()


def stationary_body(nb, nt, tokens, expert_ids, gate_values, w_gate, w_up, w_down):
    rows, features = tokens.shape
    experts, width, ff = w_gate.shape
    f32, bf16 = jnp.float32, jnp.bfloat16
    wave_rows = rows // WAVES
    block, half = nt * wave_rows, nt // 2
    dma = pltpu.SemaphoreType.DMA
    vmem = pl.BlockSpec(memory_space=pltpu.VMEM)
    anywhere = pl.BlockSpec(memory_space=pl.ANY)
    return pl.pallas_call(
        functools.partial(kernel, nb, nt),
        out_shape=jax.ShapeDtypeStruct((rows, features), bf16),
        in_specs=[anywhere, vmem, vmem, anywhere, anywhere, anywhere],
        out_specs=vmem,
        scratch_shapes=[
            pltpu.VMEM((rows, features), bf16),
            pltpu.VMEM((nb, nt, SUBLANES, LANES), f32),
            pltpu.VMEM(w_gate.shape, bf16),
            pltpu.VMEM(w_up.shape, bf16),
            pltpu.VMEM(w_down.shape, bf16),
            pltpu.VMEM((WAVES, nb, nt, wave_rows, width), bf16),
            pltpu.VMEM((WAVES, nb, block, 2 * ff), f32),
            pltpu.VMEM((WAVES, nb, block, 2 * ff), bf16),
            pltpu.VMEM((WAVES, nb, block, 2 * ff), bf16),
            pltpu.VMEM((WAVES, nb, block, ff), bf16),
            pltpu.VMEM((WAVES, nb, block, width), f32),
            pltpu.VMEM((WAVES, nb, half, wave_rows, width), f32),
            pltpu.VMEM((WAVES, nb, half, wave_rows, width), bf16),
            pltpu.VMEM((WAVES, nb, half, wave_rows, width), bf16),
            pltpu.VMEM((WAVES, nb, wave_rows, width), bf16),
            dma((5 + WAVES,)),
            dma((WAVES, nb,)), dma((WAVES, nb,)),
            dma((WAVES, nb, half)), dma((WAVES, nb, half)),
            dma((WAVES, nb,)), dma((WAVES, nb,)),
            dma((WAVES, nb, half)), dma((WAVES, nb, half)),
            dma((nb, nt)), dma((nb, nt)),
            dma((WAVES, nb, CHUNKS)), dma((WAVES, nb, CHUNKS)),
            dma((WAVES, nb, CHUNKS)), dma((WAVES, nb, CHUNKS)),
            dma((WAVES, nb, half)), dma((WAVES, nb, half)),
            dma((WAVES, nb, half)), dma((WAVES, nb, half)),
            dma((WAVES, nb,)), dma((WAVES, nb,)),
        ],
        compiler_params=pltpu.CompilerParams(collective_id=0, has_side_effects=True),
    )(tokens, expert_ids.reshape(1, rows), gate_values.reshape(1, rows), w_gate, w_up, w_down)


def solution(mesh):
    nb, nt = mesh.shape["blk"], mesh.shape["tok"]

    def body(tokens, expert_ids, gate_values, w_gate, w_up, w_down):
        rows = tokens.shape[0]
        width, ff = w_gate.shape[1], w_gate.shape[2]
        fits = width % LANES == 0 and ff % LANES == 0 and rows % (16 * WAVES) == 0 and rows <= LANES
        if fits and nt % 2 == 0 and nb == 4 and nt * rows % (16 * CHUNKS * WAVES) == 0:
            return stationary_body(nb, nt, tokens, expert_ids, gate_values, w_gate, w_up, w_down)
        return gathered_body(tokens, expert_ids, gate_values, w_gate, w_up, w_down)

    return jax.shard_map(
        body,
        mesh=mesh,
        in_specs=(
            P(("groups", "blk", "tok"), None),
            P(("groups", "blk", "tok"), None),
            P(("groups", "blk", "tok"), None),
            P(None, "blk", "tok"),
            P(None, "blk", "tok"),
            P(None, "tok", "blk"),
        ),
        out_specs=P(("groups", "blk", "tok"), None),
        check_vma=False,
    )
```

time: 74.1 us -> 70.5 us (0.951)
  Pallas kernels: 72.1 us -> 68.5 us
    pallas_call x1, Pallas kernels: 72.1 us -> 68.5 us  [stationary_body(): pl.pallas_call(functools.partial(kernel, nb, nt), out_shape=jax.ShapeDtyp...]
where the time goes in v3:
time: 70.5 us; the launch traced here: 70.3 us
  Pallas kernels  68.5 us (97%)
  local copies, waits for them, and re-layouts  1.82 us (3%)
    pallas_call x1, Pallas kernels, stationary_body(): pl.pallas_call(functools.partial(kernel, nb, nt), out_shape=jax.ShapeDtyp...  68.5 us
    unnamed x1, local copies, waits for them, and re-layouts  1.82 us

profile of v3, /device:TPU:0, one launch (start us, length us, event | category | flops | bytes accessed | tf_op | source)
XLA Modules:
  0.0 70.3 jit_solution(1015480241233868911)
XLA Ops:
  0.0 68.5 %shard_map.64 = bf16[64,3584]{1,0:T(8,128)(2,1)} custom-call(bf16[64,3584]{1,0:T(8,128)(2,1)} %tok_hbm.1, s32[1,64]{1,0:T(1,128)} %bitcast.2, f32[1,64]{1,0:T(1,128)} %bitcast.3, bf16[2,896,256]{2,1,0:T(8,128)(2,1)} %wg_hbm.1, bf16[2,896,256]{2,1,0:T(8,128)(2,1)} %wu_hbm.1, bf16[2,256,896]{2,1,0:T(8,128)(2,1)} %wd_hbm.1), custom_call_target="tpu_custom_call" | custom-call | tf_op jit(solution)/shard_map/pallas_call | solution.py:327
  68.5 1.8 %copy.8 = bf16[64,3584]{1,0:T(8,128)(2,1)} copy(bf16[64,3584]{1,0:T(8,128)(2,1)} %shard_map.64) | data formatting | bytes 917504

commit v4 on v3

--- a/solution.py
+++ b/solution.py
@@ -10,7 +10,7 @@
 LANES = 128
 SUBLANES = 8
 CHUNKS = 1
-WAVES = 2
+WAVES = 4
 
 
 def gathered_body(tokens, expert_ids, gate_values, w_gate, w_up, w_down):

time: 70.5 us -> 94 us (1.33)
  Pallas kernels: 68.5 us -> 92 us
    pallas_call x1, Pallas kernels: 68.5 us -> 92 us  [stationary_body(): pl.pallas_call(functools.partial(kernel, nb, nt), out_shape=jax.ShapeDtyp...]
where the time goes in v4:
time: 94 us; the launch traced here: 93.8 us
  Pallas kernels  92 us (98%)
  local copies, waits for them, and re-layouts  1.82 us (2%)
    pallas_call x1, Pallas kernels, stationary_body(): pl.pallas_call(functools.partial(kernel, nb, nt), out_shape=jax.ShapeDtyp...  92 us

profile of v4, /device:TPU:0, one launch (start us, length us, event | category | flops | bytes accessed | tf_op | source)
XLA Modules:
  0.0 93.8 jit_solution(11828187230368487914)
XLA Ops:
  0.0 92.0 %shard_map.64 = bf16[64,3584]{1,0:T(8,128)(2,1)} custom-call(bf16[64,3584]{1,0:T(8,128)(2,1)} %tok_hbm.1, s32[1,64]{1,0:T(1,128)} %bitcast.2, f32[1,64]{1,0:T(1,128)} %bitcast.3, bf16[2,896,256]{2,1,0:T(8,128)(2,1)} %wg_hbm.1, bf16[2,896,256]{2,1,0:T(8,128)(2,1)} %wu_hbm.1, bf16[2,256,896]{2,1,0:T(8,128)(2,1)} %wd_hbm.1), custom_call_target="tpu_custom_call" | custom-call | tf_op jit(solution)/shard_map/pallas_call | solution.py:327
  92.0 1.8 %copy.8 = bf16[64,3584]{1,0:T(8,128)(2,1)} copy(bf16[64,3584]{1,0:T(8,128)(2,1)} %shard_map.64) | data formatting | bytes 917504
